TPU v7x, 32 devices: a whole 2x2x4 slice. The times are simulated.
32 devices in a mesh: row: 4 (over y, x), col: 8 (over z, core).
Axes of the slice: x: 2, y: 2, z: 4, core: 2. Of those that a mesh axis runs over, the one named last changes fastest.
Arguments:
- left_tiles: bfloat16 [2, 32, 256, 256], P(None, 'row', 'col'), may hold values from 0.02 to 3, as said below
- right_tile_store: bfloat16 [32, 24, 256, 256], P('col', 'row'), may hold values from 0.019897461 to 1
- right_index: int32 [32, 24], P('col', 'row'), may hold values from 0 to 7, as said below
- right_count: int32 [32, 4], P('col', 'row'), may hold values from 1 to 6
Outputs:
- inflated: bfloat16 [2, 32, 256, 256], P(None, 'col', 'row')
Inputs may be any that keep to these rules, and one draw needn't show every extreme that they name: `right_index`: for each column block and each row index the 6 slots name distinct contraction blocks; only the first right_count of them are used. `left_tiles`: positive entries.
All inputs are finite; a program needn't handle non-finite values.
Results may differ from a plain program's by a relative error of at most 0.001.
Values may be sent and summed in bfloat16 or wider, within the bound.
No kernel may reach another device: no remote copies, remote signals or barrier semaphores. Data moves between devices by JAX's collectives and lax.ppermute only.
A program may use at most 64 MiB of HBM per device.

v0:
```python
import jax
import jax.numpy as jnp
from jax import lax
from jax.sharding import PartitionSpec as P


def shards(left_tiles, right_tile_store, right_index, right_count):
    column_blocks = right_tile_store.shape[0]
    slot_total = right_tile_store.shape[1]
    window_blocks = left_tiles.shape[0]
    tile_size = right_tile_store.shape[2]
    live_mask = (jnp.arange(slot_total, dtype=jnp.int32)[None, :] < right_count).astype(
        jnp.bfloat16
    )
    flat_index = right_index.reshape(-1)
    shard_rows = lax.all_gather(left_tiles, "col", axis=2, tiled=True)
    picked = jnp.take(shard_rows, flat_index, axis=1)
    picked = picked.reshape(
        window_blocks, column_blocks, slot_total, shard_rows.shape[2], shard_rows.shape[3]
    )
    picked = picked * live_mask[None, :, :, None, None]
    partial_value = jnp.einsum(
        "ajqmb,jqbn->ajmn", picked, right_tile_store, preferred_element_type=jnp.float32
    )
    share = lax.psum_scatter(partial_value, "row", scatter_dimension=2, tiled=True)
    squared = share * share
    column_sums = lax.psum(jnp.sum(squared, axis=(0, 2)), "row")
    scaled = squared * (window_blocks * tile_size / column_sums[None, :, None, :])
    return scaled.astype(jnp.bfloat16)


def solution(mesh):
    in_specs = (
        P(None, "row", "col", None),
        P("col", "row", None, None),
        P("col", "row"),
        P("col", "row"),
    )
    out_specs = P(None, "col", "row", None)
    return jax.shard_map(shards, mesh=mesh, in_specs=in_specs, out_specs=out_specs, check_vma=False)
```

profile of v0, /device:TPU:0, one launch (start us, length us, event | category | flops | bytes accessed | tf_op | source)
XLA Modules:
  0.0 106.3 jit_solution(15490569830004205076)
XLA Ops:
  6.5 0.0 copy-start
  6.5 0.0 all-gather.2.cloned.1.call-start
  6.5 0.7 all-gather.2.cloned.1.call-update
  7.3 0.0 reduce-scatter.2.cloned.1.call-start
  7.3 0.9 reshape.66
  8.3 0.8 fusion.12
  9.0 31.8 %all-gather.2.cloned.1.call-done = bf16[2,8,256,256]{3,2,1,0:T(8,128)(2,1)} async-done(((bf16[2,8,32,256]{3,2,1,0:T(8,128)(2,1)}), bf16[2,8,256,256]{3,2,1,0:T(8,128)(2,1)}) %all-gather.2.cloned.1.call-update) | async-done | bytes 2097168 | tf_op jit(solution)/shard_map/all_gather | solution.py:16
  40.8 6.0 %gather_fusion = bf16[24,2,256,256]{3,2,1,0:T(8,128)(2,1)} fusion(bf16[2,8,256,256]{3,2,1,0:T(8,128)(2,1)} %all-gather.2.cloned.1.call-done, s32[1024]{0:T(1024)S(1)} %pad_clamp_fusion), kind=kCustom, calls=%fused_computation | custom fusion | bytes 12583008 | tf_op jit(solution)/shard_map/jit(_take)/gather | solution.py:17
  46.8 0.0 copy-done
  46.8 6.0 %fusion.7 = f32[2,4,256,256]{3,2,0,1:T(8,128)} fusion(bf16[4,6,256,256]{3,2,1,0:T(8,128)(2,1)S(1)} %copy-done, bf16[2,4,6,256,256]{4,3,0,2,1:T(8,128)(2,1)} %bitcast.18, pred[4,6]{1,0:T(4,128)(4,1)S(1)} %get-tuple-element.6, bf16[4,6]{1,0:T(4,128)(2,1)S(1)} %get-tuple-element.5), kind=kOutput, calls=%fused_computation.8 | convolution fusion | flops 1616904192 | bytes 11534408 | tf_op jit(solution)/shard_map/ajqmb,jqbn->ajmn/dot_general | solution.py:22
  52.8 0.0 reduce-scatter.2.cloned.1.call-update
  52.8 34.7 %reduce-scatter.2.cloned.1.call-done = f32[2,4,64,256]{3,2,0,1:T(8,128)} async-done(((f32[2,4,256,256]{3,2,0,1:T(8,128)}), f32[2,4,64,256]{3,2,0,1:T(8,128)}) %reduce-scatter.2.cloned.1.call-update) | async-done | bytes 524304 | tf_op jit(solution)/shard_map/reduce_scatter | solution.py:25
  87.6 1.1 %multiply_reduce_fusion = f32[4,256]{1,0:T(4,128)S(1)} fusion(f32[2,4,64,256]{3,2,0,1:T(8,128)} %reduce-scatter.2.cloned.1.call-done), kind=kLoop, calls=%fused_computation.10 | loop fusion | flops 261120 | bytes 528384 | tf_op jit(solution)/shard_map/reduce_sum | solution.py:27
  88.7 9.0 %psum.7 = f32[4,256]{1,0:T(4,128)S(1)} all-reduce(f32[4,256]{1,0:T(4,128)S(1)} %multiply_reduce_fusion), channel_id=1, replica_groups=mesh['row'=4,'col'=8] {'row'}, use_global_device_ids=true, to_apply=%region_2.3 | all-reduce | flops 1024 | bytes 8192 | tf_op jit(solution)/shard_map/psum | solution.py:27
  97.6 1.1 %multiply_convert_fusion = bf16[2,4,64,256]{3,2,0,1:T(8,128)(2,1)S(1)} fusion(f32[2,4,64,256]{3,2,0,1:T(8,128)} %reduce-scatter.2.cloned.1.call-done, f32[4,256]{1,0:T(4,128)S(1)} %broadcast_divide_fusion), kind=kLoop, calls=%fused_computation.9 | loop fusion | flops 393216 | bytes 790528 | tf_op jit(solution)/shard_map/convert_element_type | solution.py:29
  98.7 0.7 copy.6
  (3 shorter events, 0.0 us)
Async XLA Ops:
  6.5 40.3 %copy-start = (bf16[4,6,256,256]{3,2,1,0:T(8,128)(2,1)S(1)}, bf16[4,6,256,256]{3,2,1,0:T(8,128)(2,1)}, u32[]{:S(2)}) copy-start(bf16[4,6,256,256]{3,2,1,0:T(8,128)(2,1)} %param.5) | copy-start | bytes 9437188
  6.5 34.3 %all-gather.2.cloned.1.call-start = ((), (), s32[]{:S(2)}) async-start(), calls=%async_computation.1 | async-start | bytes 2359296 | tf_op jit(solution)/shard_map/all_gather | solution.py:16
  7.3 80.3 %reduce-scatter.2.cloned.1.call-start = ((), (), s32[]{:S(2)}) async-start(), calls=%async_computation.2 | async-start | bytes 2621440 | tf_op jit(solution)/shard_map/reduce_scatter | solution.py:25
Sparse Core Ops, SparseCore 0:
  8.9 31.8 all-gather.1
  52.9 34.5 reduce-scatter.1
where the time goes:
time: 107 us; the launch traced here: 106 us
  waiting for transfers between devices  67.3 us (63%)
  between operations  13.4 us (13%)
  blocking collectives  8.97 us (8%)
  local copies, waits for them, and re-layouts  7.65 us (7%)
  matrix products  5.96 us (6%)
  other arithmetic  2.98 us (3%)
    reduce_scatter x1, waiting for transfers between devices, shards(): lax.psum_scatter(partial_value, 'row', scatter_dimension=2, tiled=True)  34.7 us
    all_gather x1, waiting for transfers between devices, shards(): shard_rows = lax.all_gather(left_tiles, 'col', axis=2, tiled=True)  31.8 us
    psum x1, blocking collectives, shards(): column_sums = lax.psum(jnp.sum(squared, axis=(0, 2)), 'row')  8.97 us
    gather x1, local copies, waits for them, and re-layouts, shards(): picked = jnp.take(shard_rows, flat_index, axis=1)  5.99 us
    dot_general x1, matrix products, shards(): jnp.einsum('ajqmb,jqbn->ajmn', picked, right_tile_store, preferred_elemen...  5.96 us
  transfers between devices with their start and end apart: 2, of which 2 were waited for; matrix products, arithmetic and copies ran while one was open for 2% of the time, Pallas kernels for 0%

commit v1 on v0

--- a/solution.py
+++ b/solution.py
@@ -1,7 +1,15 @@
+import functools
 import jax
 import jax.numpy as jnp
 from jax import lax
 from jax.sharding import PartitionSpec as P
+
+
+def derive_entries_in(sample, shard_axis):
+    return jnp.sum(lax.all_gather(sample, shard_axis), 0)
+
+
+solve_wall = functools.partial(derive_entries_in, shard_axis="row")
 
 
 def shards(left_tiles, right_tile_store, right_index, right_count):
@@ -24,7 +32,7 @@
     )
     share = lax.psum_scatter(partial_value, "row", scatter_dimension=2, tiled=True)
     squared = share * share
-    column_sums = lax.psum(jnp.sum(squared, axis=(0, 2)), "row")
+    column_sums = solve_wall(jnp.sum(squared, axis=(0, 2)))
     scaled = squared * (window_blocks * tile_size / column_sums[None, :, None, :])
     return scaled.astype(jnp.bfloat16)
 

time: 107 us -> 106 us (level)
    psum x1 -> x0, blocking collectives: 8.97 us -> none  [shards(): column_sums = lax.psum(jnp.sum(squared, axis=(0, 2)), 'row')]
    all_gather x0 -> x1, blocking collectives: none -> 8.16 us  [derive_entries_in(): return jnp.sum(lax.all_gather(sample, shard_axis), 0)]
where the time goes in v1:
time: 106 us
  waiting for transfers between devices  67.3 us (63%)
  between operations  13.4 us (13%)
  blocking collectives  8.16 us (8%)
  local copies, waits for them, and re-layouts  7.65 us (7%)
  matrix products  5.96 us (6%)
  other arithmetic  2.99 us (3%)
    reduce_scatter x1, waiting for transfers between devices, shards(): lax.psum_scatter(partial_value, 'row', scatter_dimension=2, tiled=True)  34.7 us
    all_gather x1, waiting for transfers between devices, shards(): shard_rows = lax.all_gather(left_tiles, 'col', axis=2, tiled=True)  31.8 us
    all_gather x1, blocking collectives, derive_entries_in(): return jnp.sum(lax.all_gather(sample, shard_axis), 0)  8.16 us
    gather x1, local copies, waits for them, and re-layouts, shards(): picked = jnp.take(shard_rows, flat_index, axis=1)  5.99 us
    dot_general x1, matrix products, shards(): jnp.einsum('ajqmb,jqbn->ajmn', picked, right_tile_store, preferred_elemen...  5.96 us
  transfers between devices with their start and end apart: 2, of which 2 were waited for; matrix products, arithmetic and copies ran while one was open for 2% of the time, Pallas kernels for 0%

profile of v1, /device:TPU:0, one launch (start us, length us, event | category | flops | bytes accessed | tf_op | source)
XLA Modules:
  0.0 105.5 jit_solution(14533464524063489275)
XLA Ops:
  6.5 0.0 copy-start
  6.5 0.0 all-gather.4.cloned.1.call-start
  6.5 0.7 all-gather.4.cloned.1.call-update
  7.3 0.0 reduce-scatter.2.cloned.1.call-start
  7.3 0.9 reshape.68
  8.3 0.8 fusion.12
  9.0 31.8 %all-gather.4.cloned.1.call-done = bf16[2,8,256,256]{3,2,1,0:T(8,128)(2,1)} async-done(((bf16[2,8,32,256]{3,2,1,0:T(8,128)(2,1)}), bf16[2,8,256,256]{3,2,1,0:T(8,128)(2,1)}) %all-gather.4.cloned.1.call-update) | async-done | bytes 2097168 | tf_op jit(solution)/shard_map/all_gather | solution.py:24
  40.8 6.0 %gather_fusion = bf16[24,2,256,256]{3,2,1,0:T(8,128)(2,1)} fusion(bf16[2,8,256,256]{3,2,1,0:T(8,128)(2,1)} %all-gather.4.cloned.1.call-done, s32[1024]{0:T(1024)S(1)} %pad_clamp_fusion), kind=kCustom, calls=%fused_computation | custom fusion | bytes 12583008 | tf_op jit(solution)/shard_map/jit(_take)/gather | solution.py:25
  46.8 0.0 copy-done
  46.8 6.0 %fusion.7 = f32[2,4,256,256]{3,2,0,1:T(8,128)} fusion(bf16[4,6,256,256]{3,2,1,0:T(8,128)(2,1)S(1)} %copy-done, bf16[2,4,6,256,256]{4,3,0,2,1:T(8,128)(2,1)} %bitcast.19, pred[4,6]{1,0:T(4,128)(4,1)S(1)} %get-tuple-element.6, bf16[4,6]{1,0:T(4,128)(2,1)S(1)} %get-tuple-element.5), kind=kOutput, calls=%fused_computation.8 | convolution fusion | flops 1616904192 | bytes 11534408 | tf_op jit(solution)/shard_map/ajqmb,jqbn->ajmn/dot_general | solution.py:30
  52.8 0.0 reduce-scatter.2.cloned.1.call-update
  52.8 34.7 %reduce-scatter.2.cloned.1.call-done = f32[2,4,64,256]{3,2,0,1:T(8,128)} async-done(((f32[2,4,256,256]{3,2,0,1:T(8,128)}), f32[2,4,64,256]{3,2,0,1:T(8,128)}) %reduce-scatter.2.cloned.1.call-update) | async-done | bytes 524304 | tf_op jit(solution)/shard_map/reduce_scatter | solution.py:33
  87.6 1.1 %multiply_reduce_fusion = f32[4,256]{1,0:T(4,128)S(1)} fusion(f32[2,4,64,256]{3,2,0,1:T(8,128)} %reduce-scatter.2.cloned.1.call-done), kind=kLoop, calls=%fused_computation.10 | loop fusion | flops 261120 | bytes 528384 | tf_op jit(solution)/shard_map/reduce_sum | solution.py:35
  88.7 8.2 %all-gather.1 = f32[4,4,256]{2,1,0:T(4,128)S(1)} all-gather(f32[1,4,256]{2,1,0:T(4,128)S(1)} %bitcast.20), channel_id=2, replica_groups=mesh['row'=4,'col'=8] {'row'}, dimensions={0}, use_global_device_ids=true | all-gather | bytes 20480 | tf_op jit(solution)/shard_map/all_gather | solution.py:9
  96.9 1.1 %multiply_convert_fusion = bf16[2,4,64,256]{3,2,0,1:T(8,128)(2,1)S(1)} fusion(f32[2,4,64,256]{3,2,0,1:T(8,128)} %reduce-scatter.2.cloned.1.call-done, f32[4,256]{1,0:T(4,128)S(1)} %broadcast_divide_fusion), kind=kLoop, calls=%fused_computation.9 | loop fusion | flops 393216 | bytes 790528 | tf_op jit(solution)/shard_map/convert_element_type | solution.py:37
  98.0 0.7 copy.8
  (4 shorter events, 0.0 us)
Async XLA Ops:
  6.5 40.3 %copy-start = (bf16[4,6,256,256]{3,2,1,0:T(8,128)(2,1)S(1)}, bf16[4,6,256,256]{3,2,1,0:T(8,128)(2,1)}, u32[]{:S(2)}) copy-start(bf16[4,6,256,256]{3,2,1,0:T(8,128)(2,1)} %param.5) | copy-start | bytes 9437188
  6.5 34.3 %all-gather.4.cloned.1.call-start = ((), (), s32[]{:S(2)}) async-start(), calls=%async_computation.1 | async-start | bytes 2359296 | tf_op jit(solution)/shard_map/all_gather | solution.py:24
  7.3 80.3 %reduce-scatter.2.cloned.1.call-start = ((), (), s32[]{:S(2)}) async-start(), calls=%async_computation.2 | async-start | bytes 2621440 | tf_op jit(solution)/shard_map/reduce_scatter | solution.py:33
Sparse Core Ops, SparseCore 0:
  8.9 31.8 all-gather.3
  52.9 34.5 reduce-scatter.1
